TPU v7x, 32 devices: a whole 2x2x4 slice. The times are simulated.
32 devices in a mesh: grp: 2 (over x), seq: 8 (over z, y), kv: 2 (over core).
Axes of the slice: x: 2, y: 2, z: 4, core: 2. Of those that a mesh axis runs over, the one named last changes fastest.
Arguments:
- queries: bfloat16 [4, 64, 128], P(('grp', 'kv'), 'seq'), parts along dimension 0, may hold values from -256 to 256
- keys: bfloat16 [4, 16384, 8, 128], P(('grp', 'kv'), 'seq'), parts along dimension 0, may hold values from -6 to 6
- values: bfloat16 [4, 16384, 8, 128], P(('grp', 'kv'), 'seq'), parts along dimension 0, may hold values from -6 to 6
- picks: int32 [4, 64, 3], P(('grp', 'kv'), 'seq'), parts along dimension 0, may hold values from 0 to 31, as said below
- lengths: int32 [4], P(('grp', 'kv')), parts along dimension 0, may hold values from 8194 to 16384, as said below
Outputs:
- attended: bfloat16 [4, 64, 128], P(('grp', 'kv'), 'seq'), parts along dimension 0
There are 2 independent parts, one for each index of `grp`. A program takes and returns all parts, laid end to end along the dimension named above; each array names one. Nothing has to cross between parts.
Inputs may be any that keep to these rules, and one draw needn't show every extreme that they name: `picks`: each row of 3 holds distinct block numbers in ascending order; the last is the block that holds position lengths[b] - 1, the others lie before it. Position lengths[b] - 1 is never the first position of its block.
All inputs are finite; a program needn't handle non-finite values.
Results may differ from a plain program's by a relative error of at most 0.0046.
Values may be sent and summed in bfloat16 or wider, within the bound.
A program may use at most 64 MiB of HBM per device.

v0:
```python
import math
import jax
import jax.numpy as jnp
from jax import lax
from jax.sharding import PartitionSpec as P

BLOCK = 512
NEGATIVE = -1e30


def shards(queries, keys, values, picks, lengths):
    rows = queries.shape[0]
    head_dim = queries.shape[2]
    local_len = keys.shape[1]
    kv_heads = keys.shape[2]
    blocks_here = local_len // BLOCK
    seq_index = lax.axis_index("seq")
    all_queries, all_picks = (
        lax.all_gather(queries, "seq", axis=1, tiled=True),
        lax.all_gather(picks, "seq", axis=1, tiled=True),
    )
    heads = all_queries.shape[1]
    group = heads // kv_heads
    grouped = all_queries.reshape(rows, kv_heads, group, head_dim)
    scores = jnp.einsum("bkgd,btkd->bkgt", grouped, keys, preferred_element_type=jnp.float32) * (
        1.0 / math.sqrt(head_dim)
    )
    scores = scores.reshape(rows, kv_heads, group, blocks_here, BLOCK)
    block_ids = seq_index * blocks_here + jnp.arange(blocks_here, dtype=jnp.int32)
    chosen = jnp.any(all_picks[:, :, :, None] == block_ids[None, None, None, :], axis=2)
    chosen = chosen.reshape(rows, kv_heads, group, blocks_here)
    positions = block_ids[:, None] * BLOCK + jnp.arange(BLOCK, dtype=jnp.int32)[None, :]
    inside = positions[None, :, :] < lengths[:, None, None]
    live = jnp.logical_and(chosen[..., None], inside[:, None, None, :, :])
    masked = jnp.where(live, scores, -jnp.inf)
    any_live = jnp.any(live, axis=-1)
    safe_max = jnp.where(any_live, jnp.max(masked, axis=-1), NEGATIVE)
    weight = jnp.exp(masked - safe_max[..., None])
    block_total = jnp.sum(weight, axis=-1)
    rounded = weight.astype(jnp.bfloat16)
    blocked_values = values.reshape(rows, blocks_here, BLOCK, kv_heads, head_dim)
    block_out = jnp.einsum(
        "bkgnt,bntkd->bkgnd", rounded, blocked_values, preferred_element_type=jnp.float32
    )
    device_max = jnp.max(safe_max, axis=-1)
    coef = jnp.exp(safe_max - device_max[..., None])
    partial_out = jnp.sum(block_out * coef[..., None], axis=3).reshape(rows, heads, head_dim)
    partial_total = jnp.sum(block_total * coef, axis=-1).reshape(rows, heads)
    partial_max = device_max.reshape(rows, heads)
    came_out, came_max, came_total = (
        lax.all_to_all(partial_out[None], "seq", split_axis=2, concat_axis=0, tiled=True),
        lax.all_to_all(partial_max[None], "seq", split_axis=2, concat_axis=0, tiled=True),
        lax.all_to_all(partial_total[None], "seq", split_axis=2, concat_axis=0, tiled=True),
    )
    top = jnp.max(came_max, axis=0)
    rescale = jnp.exp(came_max - top[None])
    mine_out = jnp.sum(came_out * rescale[..., None], axis=0)
    mine_total = jnp.sum(came_total * rescale, axis=0)
    return (mine_out / mine_total[..., None]).astype(jnp.bfloat16)


def solution(mesh):
    return jax.shard_map(
        shards,
        mesh=mesh,
        in_specs=(
            P(("grp", "kv"), "seq", None),
            P(("grp", "kv"), "seq", None, None),
            P(("grp", "kv"), "seq", None, None),
            P(("grp", "kv"), "seq", None),
            P(("grp", "kv")),
        ),
        out_specs=P(("grp", "kv"), "seq", None),
        check_vma=False,
    )
```

profile of v0, /device:TPU:0, one launch (start us, length us, event | category | flops | bytes accessed | tf_op | source)
XLA Modules:
  0.0 97.5 jit_solution(2691425866918644044)
XLA Ops:
  0.7 0.8 copy.28
  1.4 28.1 %all_gather.7 = bf16[1,64,128]{2,1,0:T(8,128)(2,1)S(1)} all-gather(bf16[1,8,128]{2,1,0:T(8,128)(2,1)} %param.5), channel_id=1, replica_groups=mesh['grp'=2,'seq'=8,'kv'=2] {'seq'}, dimensions={1}, use_global_device_ids=true | all-gather | bytes 18432 | tf_op jit(solution)/shard_map/all_gather | solution.py:19
  29.5 30.6 %all_gather.6 = s32[1,64,3]{2,0,1:T(1,128)S(1)} all-gather(s32[1,8,3]{2,0,1:T(1,128)S(1)} %copy.28), channel_id=1, replica_groups=mesh['grp'=2,'seq'=8,'kv'=2] {'seq'}, dimensions={1}, use_global_device_ids=true | all-gather | bytes 864 | tf_op jit(solution)/shard_map/all_gather | solution.py:20
  60.1 0.1 copy.29
  60.1 0.1 compare_reduce_fusion
  60.2 0.1 and.40
  60.3 0.1 add_compare_fusion
  60.4 0.7 and_reduce_fusion
  61.1 3.4 %fusion.4 = f32[8,8,2048]{2,1,0:T(8,128)S(1)} fusion(bf16[2048,8,128]{2,1,0:T(8,128)(2,1)} %bitcast.31, bf16[1,64,128]{2,1,0:T(8,128)(2,1)S(1)} %all_gather.7), kind=kOutput, calls=%fused_computation.4 | convolution fusion | flops 33685504 | bytes 4734976 | tf_op jit(solution)/shard_map/bkgd,btkd->bkgt/dot_general | solution.py:25
  64.5 0.2 fusion.16
  64.8 0.7 broadcast_in_dim_reshape.13
  65.5 3.9 %all-to-all-start.1 = ((f32[1,1,64]{1,0,2:T(1,128)}), f32[1,1,64]{1,0,2:T(1,128)S(1)}, u32[]{:S(2)}, u32[]{:S(2)}) async-start(f32[1,1,64]{1,0,2:T(1,128)} %broadcast_in_dim_reshape.13), calls=%async_computation.1 | async-start | bytes 65536 | tf_op jit(solution)/shard_map/all_to_all | solution.py:52
  69.4 0.3 exponential_reduce_fusion
  69.7 0.7 broadcast_in_dim_reshape.14
  70.4 5.6 %all-to-all-done.1 = f32[1,1,64]{1,0,2:T(1,128)S(1)} async-done(((f32[1,1,64]{1,0,2:T(1,128)}), f32[1,1,64]{1,0,2:T(1,128)S(1)}, u32[]{:S(2)}, u32[]{:S(2)}) %all-to-all-start.1) | async-done | bytes 288 | tf_op jit(solution)/shard_map/all_to_all | solution.py:52
  76.1 3.3 %all-to-all-start.2 = ((f32[1,1,64]{1,0,2:T(1,128)}), f32[1,1,64]{1,0,2:T(1,128)S(1)}, u32[]{:S(2)}, u32[]{:S(2)}) async-start(f32[1,1,64]{1,0,2:T(1,128)} %broadcast_in_dim_reshape.14), calls=%async_computation.2 | async-start | bytes 65536 | tf_op jit(solution)/shard_map/all_to_all | solution.py:53
  79.4 4.1 %fusion.13 = f32[8,8,128]{2,1,0:T(8,128)} fusion(bf16[4,512,8,128]{3,2,1,0:T(8,128)(2,1)} %bitcast.34, f32[8,8,4,512]{3,1,2,0:T(8,128)S(1)} %bitcast.30, f32[8,8,4]{1,2,0:T(4,128)S(1)} %get-tuple-element.8, pred[4,512]{1,0:T(4,128)(4,1)S(1)} %add_compare_fusion, pred[8,8,4]{1,2,0:T(4,128)(4,1)S(1)} %copy.30, f32[8,8,4]{1,2,0:T(4,128)S(1)} %get-tuple-element.6), kind=kOutput, calls=%fused_computation.7 | convolution fusion | flops 34136064 | bytes 4755712 | tf_op jit(solution)/shard_map/bkgnt,bntkd->bkgnd/dot_general | solution.py:42
  83.5 0.6 reduce.12
  84.0 0.1 all_to_all.32
  84.1 0.1 all_to_all.35
  84.2 1.9 %all-to-all-done.2 = f32[1,1,64]{1,0,2:T(1,128)S(1)} async-done(((f32[1,1,64]{1,0,2:T(1,128)}), f32[1,1,64]{1,0,2:T(1,128)S(1)}, u32[]{:S(2)}, u32[]{:S(2)}) %all-to-all-start.2) | async-done | bytes 288 | tf_op jit(solution)/shard_map/all_to_all | solution.py:53
  86.0 4.1 %all-to-all-start = ((f32[1,1,64,128]{3,1,0,2:T(1,128)}), f32[1,1,64,128]{3,1,0,2:T(1,128)S(1)}, u32[]{:S(2)}, u32[]{:S(2)}) async-start(f32[1,1,64,128]{3,1,0,2:T(1,128)} %bitcast.10), calls=%async_computation | async-start | bytes 65536 | tf_op jit(solution)/shard_map/all_to_all | solution.py:51
  90.1 0.6 reduce.13
  90.7 0.1 all_to_all.34
  90.8 6.0 %all-to-all-done = f32[1,1,64,128]{3,1,0,2:T(1,128)S(1)} async-done(((f32[1,1,64,128]{3,1,0,2:T(1,128)}), f32[1,1,64,128]{3,1,0,2:T(1,128)S(1)}, u32[]{:S(2)}, u32[]{:S(2)}) %all-to-all-start) | async-done | bytes 32800 | tf_op jit(solution)/shard_map/all_to_all | solution.py:51
  96.8 0.1 multiply_reduce_fusion
  96.9 0.7 fusion.22
  (8 shorter events, 0.1 us)
Async XLA Ops:
  65.5 10.5 %all-to-all-start.1 = ((f32[1,1,64]{1,0,2:T(1,128)}), f32[1,1,64]{1,0,2:T(1,128)S(1)}, u32[]{:S(2)}, u32[]{:S(2)}) async-start(f32[1,1,64]{1,0,2:T(1,128)} %broadcast_in_dim_reshape.13), calls=%async_computation.1 | async-start | bytes 65536 | tf_op jit(solution)/shard_map/all_to_all | solution.py:52
  76.1 10.0 %all-to-all-start.2 = ((f32[1,1,64]{1,0,2:T(1,128)}), f32[1,1,64]{1,0,2:T(1,128)S(1)}, u32[]{:S(2)}, u32[]{:S(2)}) async-start(f32[1,1,64]{1,0,2:T(1,128)} %broadcast_in_dim_reshape.14), calls=%async_computation.2 | async-start | bytes 65536 | tf_op jit(solution)/shard_map/all_to_all | solution.py:53
  86.0 10.8 %all-to-all-start = ((f32[1,1,64,128]{3,1,0,2:T(1,128)}), f32[1,1,64,128]{3,1,0,2:T(1,128)S(1)}, u32[]{:S(2)}, u32[]{:S(2)}) async-start(f32[1,1,64,128]{3,1,0,2:T(1,128)} %bitcast.10), calls=%async_computation | async-start | bytes 65536 | tf_op jit(solution)/shard_map/all_to_all | solution.py:51
where the time goes:
time: 98 us; the launch traced here: 97.5 us
  blocking collectives  58.7 us (60%)
  waiting for transfers between devices  13.5 us (14%)
  starting transfers between devices  11.3 us (12%)
  matrix products  7.44 us (8%)
  other arithmetic  3.38 us (3%)
  local copies, waits for them, and re-layouts  2.59 us (3%)
    all_gather x1, blocking collectives, shards(): lax.all_gather(picks, 'seq', axis=1, tiled=True)  30.6 us
    all_gather x1, blocking collectives, shards(): lax.all_gather(queries, 'seq', axis=1, tiled=True)  28.1 us
    all_to_all x1, waiting for transfers between devices, shards(): lax.all_to_all(partial_out[None], 'seq', split_axis=2, concat_axis=0, til...  5.99 us
    all_to_all x1, waiting for transfers between devices, shards(): lax.all_to_all(partial_max[None], 'seq', split_axis=2, concat_axis=0, til...  5.64 us
    all_to_all x1, starting transfers between devices, shards(): lax.all_to_all(partial_out[None], 'seq', split_axis=2, concat_axis=0, til...  4.09 us
    dot_general x1, matrix products, shards(): jnp.einsum('bkgnt,bntkd->bkgnd', rounded, blocked_values, preferred_eleme...  4.05 us
    all_to_all x1, starting transfers between devices, shards(): lax.all_to_all(partial_max[None], 'seq', split_axis=2, concat_axis=0, til...  3.86 us
    dot_general x1, matrix products, shards(): jnp.einsum('bkgd,btkd->bkgt', grouped, keys, preferred_element_type=jnp.f...  3.38 us
  transfers between devices with their start and end apart: 3, of which 3 were waited for; matrix products, arithmetic and copies ran while one was open for 6% of the time, Pallas kernels for 0%

commit v1 on v0

--- a/solution.py
+++ b/solution.py
@@ -6,6 +6,10 @@
 
 BLOCK = 512
 NEGATIVE = -1e30
+
+
+def lay_rates_here(w_in, link_axis):
+    return jnp.concatenate(lax.all_gather(w_in, link_axis), axis=1)
 
 
 def shards(queries, keys, values, picks, lengths):
@@ -17,7 +21,7 @@
     seq_index = lax.axis_index("seq")
     all_queries, all_picks = (
         lax.all_gather(queries, "seq", axis=1, tiled=True),
-        lax.all_gather(picks, "seq", axis=1, tiled=True),
+        lay_rates_here(picks, "seq"),
     )
     heads = all_queries.shape[1]
     group = heads // kv_heads

time: 98 us -> 92.8 us (0.947)
  blocking collectives: 58.7 us -> 54.2 us
    all_gather x1, blocking collectives: 30.6 us -> 27.9 us  [lay_rates_here(): return jnp.concatenate(lax.all_gather(w_in, link_axis), axis=1)]
    all_gather x1, blocking collectives: 28.1 us -> 26.3 us  [shards(): lax.all_gather(queries, 'seq', axis=1, tiled=True)]
  transfers between devices with their start and end apart: 3 -> 3, of which waited for: 3 -> 3; matrix products, arithmetic and copies ran while one was open for 6% -> 7% of each run, Pallas kernels for 0% -> 0%
where the time goes in v1:
time: 92.8 us; the launch traced here: 92.4 us
  blocking collectives  54.2 us (58%)
  waiting for transfers between devices  13.4 us (14%)
  starting transfers between devices  10.8 us (12%)
  matrix products  7.44 us (8%)
  other arithmetic  3.38 us (4%)
  local copies, waits for them, and re-layouts  2.52 us (3%)
    all_gather x1, blocking collectives, lay_rates_here(): return jnp.concatenate(lax.all_gather(w_in, link_axis), axis=1)  27.9 us
    all_gather x1, blocking collectives, shards(): lax.all_gather(queries, 'seq', axis=1, tiled=True)  26.3 us
    all_to_all x1, waiting for transfers between devices, shards(): lax.all_to_all(partial_out[None], 'seq', split_axis=2, concat_axis=0, til...  5.99 us
    all_to_all x1, waiting for transfers between devices, shards(): lax.all_to_all(partial_max[None], 'seq', split_axis=2, concat_axis=0, til...  5.57 us
    all_to_all x1, starting transfers between devices, shards(): lax.all_to_all(partial_out[None], 'seq', split_axis=2, concat_axis=0, til...  4.09 us
    dot_general x1, matrix products, shards(): jnp.einsum('bkgnt,bntkd->bkgnd', rounded, blocked_values, preferred_eleme...  4.05 us
    dot_general x1, matrix products, shards(): jnp.einsum('bkgd,btkd->bkgt', grouped, keys, preferred_element_type=jnp.f...  3.38 us
    all_to_all x1, starting transfers between devices, shards(): lax.all_to_all(partial_total[None], 'seq', split_axis=2, concat_axis=0, t...  3.33 us
  transfers between devices with their start and end apart: 3, of which 3 were waited for; matrix products, arithmetic and copies ran while one was open for 7% of the time, Pallas kernels for 0%

profile of v1, /device:TPU:0, one launch (start us, length us, event | category | flops | bytes accessed | tf_op | source)
XLA Modules:
  0.0 92.4 jit_solution(726402913111988964)
XLA Ops:
  0.7 0.7 copy.30
  1.3 27.9 %all-gather = s32[8,8,3]{1,2,0:T(4,128)S(1)} all-gather(s32[1,8,3]{1,2,0:T(4,128)S(1)} %copy.30), channel_id=2, replica_groups=mesh['grp'=2,'seq'=8,'kv'=2] {'seq'}, dimensions={0}, use_global_device_ids=true | all-gather | bytes 864 | tf_op jit(solution)/shard_map/all_gather | solution.py:12
  29.3 0.1 eq.23
  29.3 0.1 compare_reduce_fusion
  29.4 0.1 and.40
  29.5 26.3 %all_gather.11 = bf16[1,64,128]{2,1,0:T(8,128)(2,1)S(1)} all-gather(bf16[1,8,128]{2,1,0:T(8,128)(2,1)} %param.5), channel_id=1, replica_groups=mesh['grp'=2,'seq'=8,'kv'=2] {'seq'}, dimensions={1}, use_global_device_ids=true | all-gather | bytes 18432 | tf_op jit(solution)/shard_map/all_gather | solution.py:23
  55.8 0.1 add_compare_fusion
  55.9 0.7 and_reduce_fusion
  56.6 3.4 %fusion.4 = f32[8,8,2048]{2,1,0:T(8,128)S(1)} fusion(bf16[2048,8,128]{2,1,0:T(8,128)(2,1)} %bitcast.32, bf16[1,64,128]{2,1,0:T(8,128)(2,1)S(1)} %all_gather.11), kind=kOutput, calls=%fused_computation.4 | convolution fusion | flops 33685504 | bytes 4734976 | tf_op jit(solution)/shard_map/bkgd,btkd->bkgt/dot_general | solution.py:29
  60.0 0.2 fusion.16
  60.2 0.7 broadcast_in_dim_reshape.14
  61.0 3.3 %all-to-all-start.1 = ((f32[1,1,64]{1,0,2:T(1,128)}), f32[1,1,64]{1,0,2:T(1,128)S(1)}, u32[]{:S(2)}, u32[]{:S(2)}) async-start(f32[1,1,64]{1,0,2:T(1,128)} %broadcast_in_dim_reshape.14), calls=%async_computation.1 | async-start | bytes 65536 | tf_op jit(solution)/shard_map/all_to_all | solution.py:56
  64.3 0.3 exponential_reduce_fusion
  64.6 0.7 broadcast_in_dim_reshape.15
  65.3 5.6 %all-to-all-done.1 = f32[1,1,64]{1,0,2:T(1,128)S(1)} async-done(((f32[1,1,64]{1,0,2:T(1,128)}), f32[1,1,64]{1,0,2:T(1,128)S(1)}, u32[]{:S(2)}, u32[]{:S(2)}) %all-to-all-start.1) | async-done | bytes 288 | tf_op jit(solution)/shard_map/all_to_all | solution.py:56
  70.9 3.3 %all-to-all-start.2 = ((f32[1,1,64]{1,0,2:T(1,128)}), f32[1,1,64]{1,0,2:T(1,128)S(1)}, u32[]{:S(2)}, u32[]{:S(2)}) async-start(f32[1,1,64]{1,0,2:T(1,128)} %broadcast_in_dim_reshape.15), calls=%async_computation.2 | async-start | bytes 65536 | tf_op jit(solution)/shard_map/all_to_all | solution.py:57
  74.3 4.1 %fusion.13 = f32[8,8,128]{2,1,0:T(8,128)} fusion(bf16[4,512,8,128]{3,2,1,0:T(8,128)(2,1)} %bitcast.34, f32[8,8,4,512]{3,1,2,0:T(8,128)S(1)} %bitcast.31, f32[8,8,4]{1,2,0:T(4,128)S(1)} %get-tuple-element.8, pred[4,512]{1,0:T(4,128)(4,1)S(1)} %add_compare_fusion, pred[8,8,4]{1,2,0:T(4,128)(4,1)S(1)} %copy.32, f32[8,8,4]{1,2,0:T(4,128)S(1)} %get-tuple-element.6), kind=kOutput, calls=%fused_computation.7 | convolution fusion | flops 34136064 | bytes 4755712 | tf_op jit(solution)/shard_map/bkgnt,bntkd->bkgnd/dot_general | solution.py:46
  78.3 0.6 reduce.12
  78.9 0.1 all_to_all.32
  78.9 0.1 all_to_all.35
  79.0 1.9 %all-to-all-done.2 = f32[1,1,64]{1,0,2:T(1,128)S(1)} async-done(((f32[1,1,64]{1,0,2:T(1,128)}), f32[1,1,64]{1,0,2:T(1,128)S(1)}, u32[]{:S(2)}, u32[]{:S(2)}) %all-to-all-start.2) | async-done | bytes 288 | tf_op jit(solution)/shard_map/all_to_all | solution.py:57
  80.9 4.1 %all-to-all-start = ((f32[1,1,64,128]{3,1,0,2:T(1,128)}), f32[1,1,64,128]{3,1,0,2:T(1,128)S(1)}, u32[]{:S(2)}, u32[]{:S(2)}) async-start(f32[1,1,64,128]{3,1,0,2:T(1,128)} %bitcast.9), calls=%async_computation | async-start | bytes 65536 | tf_op jit(solution)/shard_map/all_to_all | solution.py:55
  85.0 0.6 reduce.13
  85.5 0.1 all_to_all.34
  85.7 6.0 %all-to-all-done = f32[1,1,64,128]{3,1,0,2:T(1,128)S(1)} async-done(((f32[1,1,64,128]{3,1,0,2:T(1,128)}), f32[1,1,64,128]{3,1,0,2:T(1,128)S(1)}, u32[]{:S(2)}, u32[]{:S(2)}) %all-to-all-start) | async-done | bytes 32800 | tf_op jit(solution)/shard_map/all_to_all | solution.py:55
  91.7 0.1 multiply_reduce_fusion
  91.7 0.7 fusion.22
  (9 shorter events, 0.1 us)
Async XLA Ops:
  61.0 10.0 %all-to-all-start.1 = ((f32[1,1,64]{1,0,2:T(1,128)}), f32[1,1,64]{1,0,2:T(1,128)S(1)}, u32[]{:S(2)}, u32[]{:S(2)}) async-start(f32[1,1,64]{1,0,2:T(1,128)} %broadcast_in_dim_reshape.14), calls=%async_computation.1 | async-start | bytes 65536 | tf_op jit(solution)/shard_map/all_to_all | solution.py:56
  70.9 10.0 %all-to-all-start.2 = ((f32[1,1,64]{1,0,2:T(1,128)}), f32[1,1,64]{1,0,2:T(1,128)S(1)}, u32[]{:S(2)}, u32[]{:S(2)}) async-start(f32[1,1,64]{1,0,2:T(1,128)} %broadcast_in_dim_reshape.15), calls=%async_computation.2 | async-start | bytes 65536 | tf_op jit(solution)/shard_map/all_to_all | solution.py:57
  80.9 10.8 %all-to-all-start = ((f32[1,1,64,128]{3,1,0,2:T(1,128)}), f32[1,1,64,128]{3,1,0,2:T(1,128)S(1)}, u32[]{:S(2)}, u32[]{:S(2)}) async-start(f32[1,1,64,128]{3,1,0,2:T(1,128)} %bitcast.9), calls=%async_computation | async-start | bytes 65536 | tf_op jit(solution)/shard_map/all_to_all | solution.py:55
